TPU v7x, 32 devices: a whole 2x2x4 slice. The times are simulated.
32 devices in a mesh: row: 4 (over y, x), col: 8 (over z, core).
Axes of the slice: x: 2, y: 2, z: 4, core: 2. Of those that a mesh axis runs over, the one named last changes fastest.
Arguments:
- coarse_left: float32 [32, 16384], P('col', 'row'), may hold values from -3 to 3
- coarse_right: float32 [32, 16384], P('row', 'col'), may hold values from -3 to 3
- stencil_left: int32 [65536], P('row'), may hold values from -1 to 16384, as said below
- weights_left: float32 [4, 65536], P(None, 'row'), may hold values from 0.1 to 0.6
- stencil_right: int32 [65536], P('col'), may hold values from -1 to 16384, as said below
- weights_right: float32 [4, 65536], P(None, 'col'), may hold values from 0.1 to 0.6
- tile_mask: int32 [16, 16], P('row', 'col'), may hold values 0 or 1
- sample_rows: int32 [16, 16, 2048], P('row', 'col'), may hold values from 0 to 4095
- sample_cols: int32 [16, 16, 2048], P('row', 'col'), may hold values from 0 to 4095
- sample_values: float32 [16, 16, 2048], P('row', 'col'), may hold values from -6 to 6
Outputs:
- left_new: float32 [32, 65536], P('col', 'row')
- right_new: float32 [32, 65536], P('row', 'col')
Inputs may be any that keep to these rules, and one draw needn't show every extreme that they name: stencil_left[i] is i // 4 - 1, i // 4 or i // 4 + 1. stencil_right[j] is j // 4 - 1, j // 4 or j // 4 + 1.
All inputs are finite; a program needn't handle non-finite values. No bound on the sum of `tile_mask` on one device may be relied on, other than what follows from the above.
Results may differ from a plain program's by a relative error of at most 0.0001.
Values sent between devices are 32-bit elements; how exact they have to be, the bound alone decides.
No kernel may reach another device: no remote copies, remote signals or barrier semaphores. Data moves between devices by JAX's collectives and lax.ppermute only.
A program may use at most 128 MiB of HBM per device.

v0:
```python
import jax
import jax.numpy as jnp
from jax import lax
from jax.sharding import PartitionSpec as P

TILES = 16
TILE = 4096
SPT = 2048


def with_halo(block, sides, width):
    for axis, dim in sides:
        count = lax.axis_size(axis)
        forward = [(i, i + 1) for i in range(count - 1)]
        backward = [(target, source) for source, target in forward]
        low = lax.ppermute(
            lax.slice_in_dim(block, block.shape[dim] - width, None, axis=dim), axis, forward
        )
        high = lax.ppermute(lax.slice_in_dim(block, 0, width, axis=dim), axis, backward)
        block = jnp.concatenate([low, block, high], axis=dim)
    return block


def spread(padded, base, weights, offset):
    start_at = base - offset + 2
    columns_at = start_at[None, :] + jnp.arange(4, dtype=jnp.int32)[:, None]
    values = jnp.take(padded, columns_at, axis=1)
    return jnp.sum(values * weights[None], axis=1)


def on_device(
    coarse_left,
    coarse_right,
    stencil_left,
    weights_left,
    stencil_right,
    weights_right,
    tile_mask,
    sample_rows,
    sample_cols,
    sample_values,
):
    left_offset = lax.axis_index("row") * coarse_left.shape[1]
    right_offset = lax.axis_index("col") * coarse_right.shape[1]
    left_padded = with_halo(coarse_left, (("row", 1),), 3)
    left_own = spread(left_padded, stencil_left, weights_left, left_offset)
    fine_left = lax.all_gather(left_own, "col", axis=0, tiled=True)
    right_padded = with_halo(coarse_right, (("col", 1),), 3)
    right_own = spread(right_padded, stencil_right, weights_right, right_offset)
    fine_right = lax.all_gather(right_own, "row", axis=0, tiled=True)
    tile_rows, tile_cols, samples = sample_rows.shape
    row_base = (jnp.arange(tile_rows, dtype=jnp.int32) * TILE)[:, None, None]
    col_base = (jnp.arange(tile_cols, dtype=jnp.int32) * TILE)[None, :, None]
    count = tile_rows * tile_cols * samples
    width = min(count, 4096)
    blocks = count // width
    rows_all = (sample_rows + row_base).reshape(blocks, width)
    cols_all = (sample_cols + col_base).reshape(blocks, width)
    values_all = sample_values.reshape(blocks, width)
    keeping = jnp.broadcast_to(
        tile_mask[:, :, None].astype(jnp.float32), sample_values.shape
    ).reshape(blocks, width)

    def visit(carry, block):
        grad_left, grad_right = carry
        rows_here, cols_here, values_here, keep_here = block
        left_cols = jnp.take(fine_left, rows_here, axis=1)
        right_cols = jnp.take(fine_right, cols_here, axis=1)
        error = keep_here * (jnp.sum(left_cols * right_cols, axis=0) - values_here)
        grad_left = grad_left.at[:, rows_here].add(error[None, :] * right_cols)
        grad_right = grad_right.at[:, cols_here].add(error[None, :] * left_cols)
        return ((grad_left, grad_right), None)

    left_zero = jnp.zeros(fine_left.shape, jnp.float32)
    right_zero = jnp.zeros(fine_right.shape, jnp.float32)
    (grad_left, grad_right), _ = lax.scan(
        visit, (left_zero, right_zero), (rows_all, cols_all, values_all, keeping)
    )
    left_mine = lax.psum_scatter(grad_left, "col", scatter_dimension=0, tiled=True)
    right_mine = lax.psum_scatter(grad_right, "row", scatter_dimension=0, tiled=True)
    step_size = 4.0 * TILE / (SPT * TILES)
    return (left_own - step_size * left_mine, right_own - step_size * right_mine)


def solution(mesh):
    in_specs = (
        P("col", "row"),
        P("row", "col"),
        P("row"),
        P(None, "row"),
        P("col"),
        P(None, "col"),
        P("row", "col"),
        P("row", "col", None),
        P("row", "col", None),
        P("row", "col", None),
    )
    out_specs = (P("col", "row"), P("row", "col"))
    return jax.shard_map(
        on_device, mesh=mesh, in_specs=in_specs, out_specs=out_specs, check_vma=False
    )
```

profile of v0, /device:TPU:0, one launch (start us, length us, event | category | flops | bytes accessed | tf_op | source)
XLA Modules:
  0.0 962.5 jit_solution(5150380083610926015)
XLA Ops:
  8.0 4.9 collective-permute-start
  21.5 217.1 %gather_fusion.2 = f32[65536,4]{1,0:T(8,128)} fusion(f32[4,4102]{0,1:T(8,128)S(1)} %copy.62, s32[65536]{0:T(1024)S(1)} %broadcast_clamp_fusion.2), kind=kCustom, calls=%fused_computation.2 | custom fusion | bytes 2359296 | tf_op jit(solution)/shard_map/jit(_take)/gather | solution.py:27
  239.0 108.9 %gather_fusion.3 = f32[32768,8]{1,0:T(8,128)} fusion(f32[8,2054]{0,1:T(8,128)S(1)} %copy.65, s32[32768]{0:T(1024)S(1)} %broadcast_clamp_fusion.3), kind=kCustom, calls=%fused_computation.3 | custom fusion | bytes 2228224 | tf_op jit(solution)/shard_map/jit(_take)/gather | solution.py:27
  347.9 14.9 %multiply_reduce_fusion.2 = f32[8192,8]{1,0:T(8,128)} fusion(f32[4,8192,8]{2,1,0:T(8,128)} %bitcast.54, f32[4,8192]{1,0:T(4,128)S(1)} %copy-done.3, pred[4,8192]{1,0:T(4,128)(4,1)S(1)} %fusion.20), kind=kLoop, calls=%fused_computation.31 | loop fusion | flops 720896 | bytes 1474560 | tf_op jit(solution)/shard_map/reduce_sum | solution.py:28
  366.4 27.8 %multiply_reduce_fusion.1 = f32[16384,4]{1,0:T(8,128)} fusion(f32[4,16384,4]{2,1,0:T(8,128)} %bitcast.53, f32[4,16384]{1,0:T(4,128)S(1)} %copy-done.2, pred[4,16384]{1,0:T(4,128)(4,1)S(1)} %fusion.16), kind=kLoop, calls=%fused_computation.30 | loop fusion | flops 720896 | bytes 1638400 | tf_op jit(solution)/shard_map/reduce_sum | solution.py:28
  394.2 6.0 copy.63
  404.7 30.0 %all-gather.6.cloned.1.call-done = f32[8,4,16384]{2,1,0:T(4,128)} async-done(((f32[1,4,16384]{2,1,0:T(4,128)}), f32[8,4,16384]{2,1,0:T(4,128)}) %all-gather.6.cloned.1.call-update) | async-done | bytes 2097168 | tf_op jit(solution)/shard_map/all_gather | solution.py:47
  436.7 4.7 copy.67
  447.1 384.0 %while.12 = (s32[]{:T(128)}, f32[32,16384]{0,1:T(8,128)}, f32[32,8192]{0,1:T(8,128)}, s32[4,4096]{1,0:T(4,128)S(1)}, f32[4,4096]{1,0:T(4,128)S(1)}, /*index=5*/f...) while((s32[]{:T(128)}, f32[32,16384]{0,1:T(8,128)}, ...), condition=%wide.region_6.7_spmd, body=%wide.region_2.0_spmd.sunk | while | flops 1396738 | bytes 10855541 | solution.py:76
  447.2 13.0 %gather_fusion = f32[4096,32]{1,0:T(8,128)S(1)} fusion(f32[32,8192]{0,1:T(8,128)} %get-tuple-element.221, s32[4096]{0:T(1024)S(1)} %broadcast_clamp_fusion.6), kind=kCustom, calls=%fused_computation.1.clone.1 | custom fusion | bytes 1064960 | tf_op jit(solution)/shard_map/while/body/eval_jaxpr/jit(_take)/gather | solution.py:68
  460.2 17.6 %gather_fusion.1 = f32[4096,32]{1,0:T(8,128)} fusion(f32[32,16384]{0,1:T(8,128)} %get-tuple-element.219, s32[4096]{0:T(1024)S(1)} %broadcast_clamp_fusion.7), kind=kCustom, calls=%fused_computation.clone.1 | custom fusion | bytes 1064960 | tf_op jit(solution)/shard_map/while/body/eval_jaxpr/jit(_take)/gather | solution.py:67
  477.8 3.7 multiply_reduce_fusion.4
  481.5 31.8 %scatter_custom_fusion.10 = f32[32,16384]{0,1:T(8,128)} fusion(f32[32,16384]{0,1:T(8,128)} %get-tuple-element.204, s32[4096]{0:T(1024)S(1)} %bitcast.65, f32[4096,32]{1,0:T(8,128)S(1)} %gather_fusion, f32[4096]{0:T(1024)S(1)} %bitcast.55, f32[]{:T(128)} %constant.49.clone.2..sunk, pred[4096]{0:T(1024)(128)(4,1)S(1)} %compare_and_fusion.4), kind=kCustom, calls=%fused_computation.8.clone.1 | custom fusion | flops 393216 | bytes 4215296 | tf_op jit(solution)/shard_map/while/body/eval_jaxpr/scatter-add | solution.py:70
  513.4 29.8 %scatter_custom_fusion.11 = f32[32,8192]{0,1:T(8,128)} fusion(f32[32,8192]{0,1:T(8,128)} %get-tuple-element.205, s32[4096]{0:T(1024)S(1)} %bitcast.63, f32[4096,32]{1,0:T(8,128)} %gather_fusion.1, f32[4096]{0:T(1024)S(1)} %bitcast.56, f32[]{:T(128)} %constant.49.clone.2..sunk, pred[4096]{0:T(1024)(128)(4,1)S(1)} %compare_and_fusion.5), kind=kCustom, calls=%fused_computation.6.clone.1 | custom fusion | flops 393216 | bytes 3166720 | tf_op jit(solution)/shard_map/while/body/eval_jaxpr/scatter-add | solution.py:71
  543.2 13.0 %gather_fusion = f32[4096,32]{1,0:T(8,128)S(1)} fusion(f32[32,8192]{0,1:T(8,128)} %get-tuple-element.221, s32[4096]{0:T(1024)S(1)} %broadcast_clamp_fusion.6), kind=kCustom, calls=%fused_computation.1.clone.1 | custom fusion | bytes 1064960 | tf_op jit(solution)/shard_map/while/body/eval_jaxpr/jit(_take)/gather | solution.py:68
  556.2 17.6 %gather_fusion.1 = f32[4096,32]{1,0:T(8,128)} fusion(f32[32,16384]{0,1:T(8,128)} %get-tuple-element.219, s32[4096]{0:T(1024)S(1)} %broadcast_clamp_fusion.7), kind=kCustom, calls=%fused_computation.clone.1 | custom fusion | bytes 1064960 | tf_op jit(solution)/shard_map/while/body/eval_jaxpr/jit(_take)/gather | solution.py:67
  573.8 3.7 multiply_reduce_fusion.4
  577.5 31.8 %scatter_custom_fusion.10 = f32[32,16384]{0,1:T(8,128)} fusion(f32[32,16384]{0,1:T(8,128)} %get-tuple-element.204, s32[4096]{0:T(1024)S(1)} %bitcast.65, f32[4096,32]{1,0:T(8,128)S(1)} %gather_fusion, f32[4096]{0:T(1024)S(1)} %bitcast.55, f32[]{:T(128)} %constant.49.clone.2..sunk, pred[4096]{0:T(1024)(128)(4,1)S(1)} %compare_and_fusion.4), kind=kCustom, calls=%fused_computation.8.clone.1 | custom fusion | flops 393216 | bytes 4215296 | tf_op jit(solution)/shard_map/while/body/eval_jaxpr/scatter-add | solution.py:70
  609.3 29.8 %scatter_custom_fusion.11 = f32[32,8192]{0,1:T(8,128)} fusion(f32[32,8192]{0,1:T(8,128)} %get-tuple-element.205, s32[4096]{0:T(1024)S(1)} %bitcast.63, f32[4096,32]{1,0:T(8,128)} %gather_fusion.1, f32[4096]{0:T(1024)S(1)} %bitcast.56, f32[]{:T(128)} %constant.49.clone.2..sunk, pred[4096]{0:T(1024)(128)(4,1)S(1)} %compare_and_fusion.5), kind=kCustom, calls=%fused_computation.6.clone.1 | custom fusion | flops 393216 | bytes 3166720 | tf_op jit(solution)/shard_map/while/body/eval_jaxpr/scatter-add | solution.py:71
  639.2 13.0 %gather_fusion = f32[4096,32]{1,0:T(8,128)S(1)} fusion(f32[32,8192]{0,1:T(8,128)} %get-tuple-element.221, s32[4096]{0:T(1024)S(1)} %broadcast_clamp_fusion.6), kind=kCustom, calls=%fused_computation.1.clone.1 | custom fusion | bytes 1064960 | tf_op jit(solution)/shard_map/while/body/eval_jaxpr/jit(_take)/gather | solution.py:68
  652.2 17.6 %gather_fusion.1 = f32[4096,32]{1,0:T(8,128)} fusion(f32[32,16384]{0,1:T(8,128)} %get-tuple-element.219, s32[4096]{0:T(1024)S(1)} %broadcast_clamp_fusion.7), kind=kCustom, calls=%fused_computation.clone.1 | custom fusion | bytes 1064960 | tf_op jit(solution)/shard_map/while/body/eval_jaxpr/jit(_take)/gather | solution.py:67
  669.8 3.7 multiply_reduce_fusion.4
  673.5 31.8 %scatter_custom_fusion.10 = f32[32,16384]{0,1:T(8,128)} fusion(f32[32,16384]{0,1:T(8,128)} %get-tuple-element.204, s32[4096]{0:T(1024)S(1)} %bitcast.65, f32[4096,32]{1,0:T(8,128)S(1)} %gather_fusion, f32[4096]{0:T(1024)S(1)} %bitcast.55, f32[]{:T(128)} %constant.49.clone.2..sunk, pred[4096]{0:T(1024)(128)(4,1)S(1)} %compare_and_fusion.4), kind=kCustom, calls=%fused_computation.8.clone.1 | custom fusion | flops 393216 | bytes 4215296 | tf_op jit(solution)/shard_map/while/body/eval_jaxpr/scatter-add | solution.py:70
  705.3 29.8 %scatter_custom_fusion.11 = f32[32,8192]{0,1:T(8,128)} fusion(f32[32,8192]{0,1:T(8,128)} %get-tuple-element.205, s32[4096]{0:T(1024)S(1)} %bitcast.63, f32[4096,32]{1,0:T(8,128)} %gather_fusion.1, f32[4096]{0:T(1024)S(1)} %bitcast.56, f32[]{:T(128)} %constant.49.clone.2..sunk, pred[4096]{0:T(1024)(128)(4,1)S(1)} %compare_and_fusion.5), kind=kCustom, calls=%fused_computation.6.clone.1 | custom fusion | flops 393216 | bytes 3166720 | tf_op jit(solution)/shard_map/while/body/eval_jaxpr/scatter-add | solution.py:71
  735.2 13.0 %gather_fusion = f32[4096,32]{1,0:T(8,128)S(1)} fusion(f32[32,8192]{0,1:T(8,128)} %get-tuple-element.221, s32[4096]{0:T(1024)S(1)} %broadcast_clamp_fusion.6), kind=kCustom, calls=%fused_computation.1.clone.1 | custom fusion | bytes 1064960 | tf_op jit(solution)/shard_map/while/body/eval_jaxpr/jit(_take)/gather | solution.py:68
  748.2 17.6 %gather_fusion.1 = f32[4096,32]{1,0:T(8,128)} fusion(f32[32,16384]{0,1:T(8,128)} %get-tuple-element.219, s32[4096]{0:T(1024)S(1)} %broadcast_clamp_fusion.7), kind=kCustom, calls=%fused_computation.clone.1 | custom fusion | bytes 1064960 | tf_op jit(solution)/shard_map/while/body/eval_jaxpr/jit(_take)/gather | solution.py:67
  765.8 3.7 multiply_reduce_fusion.4
  769.5 31.8 %scatter_custom_fusion.10 = f32[32,16384]{0,1:T(8,128)} fusion(f32[32,16384]{0,1:T(8,128)} %get-tuple-element.204, s32[4096]{0:T(1024)S(1)} %bitcast.65, f32[4096,32]{1,0:T(8,128)S(1)} %gather_fusion, f32[4096]{0:T(1024)S(1)} %bitcast.55, f32[]{:T(128)} %constant.49.clone.2..sunk, pred[4096]{0:T(1024)(128)(4,1)S(1)} %compare_and_fusion.4), kind=kCustom, calls=%fused_computation.8.clone.1 | custom fusion | flops 393216 | bytes 4215296 | tf_op jit(solution)/shard_map/while/body/eval_jaxpr/scatter-add | solution.py:70
  801.3 29.8 %scatter_custom_fusion.11 = f32[32,8192]{0,1:T(8,128)} fusion(f32[32,8192]{0,1:T(8,128)} %get-tuple-element.205, s32[4096]{0:T(1024)S(1)} %bitcast.63, f32[4096,32]{1,0:T(8,128)} %gather_fusion.1, f32[4096]{0:T(1024)S(1)} %bitcast.56, f32[]{:T(128)} %constant.49.clone.2..sunk, pred[4096]{0:T(1024)(128)(4,1)S(1)} %compare_and_fusion.5), kind=kCustom, calls=%fused_computation.6.clone.1 | custom fusion | flops 393216 | bytes 3166720 | tf_op jit(solution)/shard_map/while/body/eval_jaxpr/scatter-add | solution.py:71
  837.4 6.3 copy.69
  843.7 43.1 %all-reduce.7.cloned.1.call-done = f32[32,8192]{1,0:T(8,128)} async-done(((f32[32,8192]{1,0:T(8,128)}), f32[32,8192]{1,0:T(8,128)}) %all-reduce.7.cloned.1.call-update) | async-done | bytes 1048592
  888.4 65.7 %all-reduce.5.cloned.1.call-done = f32[32,16384]{1,0:T(8,128)} async-done(((f32[32,16384]{1,0:T(8,128)}), f32[32,16384]{1,0:T(8,128)}) %all-reduce.5.cloned.1.call-update) | async-done | bytes 2097168
  (99 shorter events, 34.5 us)
Async XLA Ops:
  7.2 394.0 %all-gather.4.cloned.1.call-start = ((), (), s32[]{:S(2)}) async-start(), calls=%async_computation | async-start | bytes 1310720 | tf_op jit(solution)/shard_map/all_gather | solution.py:50
  8.0 11.8 %collective-permute-start = (f32[4,3]{1,0:T(4,128)S(1)}, f32[4,3]{1,0:T(4,128)S(1)}, u32[]{:S(2)}, u32[]{:S(2)}) collective-permute-start(f32[4,3]{1,0:T(4,128)S(1)} %get-tuple-element.128), channel_id=1, source_target_pairs={{0,8},{8,16},{16,24},{1,9},{9,17},{17,25},{2,10},{10,18},{18,26},{... | collective-permute-start | bytes 152 | tf_op jit(solution)/shard_map/ppermute | solution.py:16
  12.8 7.0 collective-permute-start.1
  14.9 223.6 %collective-permute-start.2 = (f32[8,3]{1,0:T(8,128)S(1)}, f32[8,3]{1,0:T(8,128)S(1)}, u32[]{:S(2)}, u32[]{:S(2)}) collective-permute-start(f32[8,3]{1,0:T(8,128)S(1)} %get-tuple-element.126), channel_id=1, source_target_pairs={{0,1},{1,2},{2,3},{3,4},{4,5},{5,6},{6,7},{8,9},{9,10},{10,11},{11... | collective-permute-start | bytes 296 | tf_op jit(solution)/shard_map/ppermute | solution.py:16
  16.4 222.2 %collective-permute-start.3 = (f32[8,3]{1,0:T(8,128)S(1)}, f32[8,3]{1,0:T(8,128)S(1)}, u32[]{:S(2)}, u32[]{:S(2)}) collective-permute-start(f32[8,3]{1,0:T(8,128)S(1)} %get-tuple-element.125), channel_id=1, source_target_pairs={{1,0},{2,1},{3,2},{4,3},{5,4},{6,5},{7,6},{9,8},{10,9},{11,10},{12... | collective-permute-start | bytes 296 | tf_op jit(solution)/shard_map/ppermute | solution.py:19
  21.5 217.1 %copy-start.4 = (f32[8,2048]{1,0:T(8,128)S(1)}, f32[8,2048]{1,0:T(8,128)}, u32[]{:S(2)}) copy-start(f32[8,2048]{1,0:T(8,128)} %param.13) | copy-start | bytes 196612
  239.0 108.9 %copy-start.3 = (f32[4,8192]{1,0:T(4,128)S(1)}, f32[4,8192]{1,0:T(4,128)}, u32[]{:S(2)}) copy-start(f32[4,8192]{1,0:T(4,128)} %param.17) | copy-start | bytes 393220
  362.8 3.6 copy-start.2
  366.3 68.4 %all-gather.6.cloned.1.call-start = ((), (), s32[]{:S(2)}) async-start(), calls=%async_computation.1 | async-start | bytes 2359296 | tf_op jit(solution)/shard_map/all_gather | solution.py:47
  394.2 6.2 copy-start.8
  394.2 6.5 copy-start.5
  394.2 6.7 copy-start.6
  394.2 6.8 copy-start.7
  400.2 486.5 %all-reduce.7.cloned.1.call-start = ((), (), s32[]{:S(2)}) async-start(), calls=%async_computation.3 | async-start | bytes 2097152
  831.1 3.7 copy-start.10
  831.1 4.4 copy-start.9
  834.8 119.3 %all-reduce.5.cloned.1.call-start = ((), (), s32[]{:S(2)}) async-start(), calls=%async_computation.2 | async-start | bytes 4194304
  837.4 49.4 %copy-start = (f32[8192,8]{0,1:T(8,128)S(1)}, f32[8192,8]{0,1:T(8,128)}, u32[]{:S(2)}) copy-start(f32[8192,8]{0,1:T(8,128)} %copy.66) | copy-start | bytes 786436
  837.4 116.7 %copy-start.1 = (f32[16384,4]{0,1:T(4,128)S(1)}, f32[16384,4]{0,1:T(4,128)}, u32[]{:S(2)}) copy-start(f32[16384,4]{0,1:T(4,128)} %copy.63) | copy-start | bytes 786436
Sparse Core Ops, SparseCore 0:
  366.5 31.7 all-gather.3
  400.4 34.3 all-gather.5
  834.9 51.8 all-reduce.6
  889.0 65.0 all-reduce.4
where the time goes:
time: 964 us; the launch traced here: 962 us
  local copies, waits for them, and re-layouts  489 us (51%)
  other arithmetic  310 us (32%)
  waiting for transfers between devices  139 us (14%)
  between operations  15.4 us (2%)
    gather x2, local copies, waits for them, and re-layouts, spread(): values = jnp.take(padded, columns_at, axis=1)  326 us
    scatter-add x4, other arithmetic, visit(): grad_left = grad_left.at[:, rows_here].add(error[None, :] * right_cols)  127 us
    scatter-add x4, other arithmetic, visit(): grad_right = grad_right.at[:, cols_here].add(error[None, :] * left_cols)  119 us
    unnamed x6, waiting for transfers between devices  109 us
    gather x4, local copies, waits for them, and re-layouts, visit(): left_cols = jnp.take(fine_left, rows_here, axis=1)  70.3 us
    gather x4, local copies, waits for them, and re-layouts, visit(): right_cols = jnp.take(fine_right, cols_here, axis=1)  51.8 us
    reduce_sum x2, other arithmetic, spread(): return jnp.sum(values * weights[None], axis=1)  42.7 us
    all_gather x1, waiting for transfers between devices, on_device(): fine_left = lax.all_gather(left_own, 'col', axis=0, tiled=True)  30 us
  transfers between devices with their start and end apart: 8, of which 3 were waited for; matrix products, arithmetic and copies ran while one was open for 28% of the time, Pallas kernels for 0%

commit v1 on v0

v1 whole, which is shorter than its diff:
```python
import functools

import jax
import jax.numpy as jnp
from jax import lax
from jax.experimental import pallas as pl
from jax.experimental.pallas import tpu as pltpu
from jax.sharding import PartitionSpec as P

TILES = 16
TILE = 4096
SPT = 2048
TAPS = 4
LOW = 2
HIGH = 3
CHUNK = 256
READ = 1024
ADD = 1024


def with_edges(block, axis):
    count = lax.axis_size(axis)
    width = block.shape[1]
    forward = [(i, i + 1) for i in range(count - 1)]
    backward = [(target, source) for source, target in forward]
    low = lax.ppermute(block[:, width - LOW :], axis, forward)
    high = lax.ppermute(block[:, :HIGH], axis, backward)
    filler = jnp.zeros((block.shape[0], 128 - LOW - HIGH), jnp.float32)
    return jnp.concatenate([low, block, high, filler], axis=1)


def split(values):
    high = values.astype(jnp.bfloat16)
    return high, (values - high.astype(jnp.float32)).astype(jnp.bfloat16)


def interpolate(padded, stencil, weights, table, out, first, last, offset, tile):
    rank = padded.shape[0]
    rows = lax.broadcasted_iota(jnp.int32, (rank, 128), 0)
    own = (rows >= first) & (rows < last)

    def group(g, _):
        column = pl.multiple_of(tile * TILE + g * 1024, 1024)
        start = pl.multiple_of(tile * (TILE // 4) + g * 256, 256)
        base = stencil[tile * (TILE // 1024) + g] - (offset + start - 1)
        window = padded[:, pl.ds(start, 384)]
        for u in range(8):
            low = 128 * (u // 4) + (64 if u % 4 == 3 else 0)
            part = window[:, low : low + 128]
            total = None
            for t in range(TAPS):
                at = jnp.broadcast_to(base[u : u + 1, :] + (t - low), (rank, 128))
                taken = jnp.take_along_axis(part, at, axis=1, mode="promise_in_bounds")
                term = taken * weights[t : t + 1, pl.ds(column + 128 * u, 128)]
                total = term if total is None else total + term
            high, rest = split(total)
            to = pl.ds(pl.multiple_of((g * 4 + u // 2) * rank, rank), rank)
            lane = (u % 2) * 128
            table[tile, to, lane : lane + 128] = high
            table[tile, to, CHUNK + lane : CHUNK + lane + 128] = rest
            out[:, pl.ds(column + 128 * u, 128)] = jnp.where(own, total, 0.0)
        return 0

    lax.fori_loop(0, TILE // 1024, group, 0)


def one_hot(index):
    lanes = lax.broadcasted_iota(jnp.int32, (CHUNK, index.shape[1]), 0)
    return jnp.where(lanes == (index & (CHUNK - 1)), 1.0, 0.0).astype(jnp.bfloat16)


def read(table, index, rank):
    hot = one_hot(index)
    found = jnp.dot(
        table, jnp.concatenate([hot, hot], axis=0), preferred_element_type=jnp.float32
    )
    chunk = jnp.broadcast_to(index >> 8, (rank, index.shape[1]))
    taken = found[:rank]
    for c in range(1, found.shape[0] // rank):
        taken = jnp.where(chunk == c, found[c * rank : (c + 1) * rank], taken)
    return taken


def add(out, values, index, tile):
    rank = values.shape[0]
    hot = one_hot(index)
    chunk = jnp.broadcast_to(index >> 8, values.shape)
    high, rest = split(values)
    zero = jnp.zeros(values.shape, jnp.bfloat16)
    left = jnp.concatenate(
        [
            jnp.concatenate(
                [jnp.where(chunk == c, high, zero), jnp.where(chunk == c, rest, zero)], axis=1
            )
            for c in range(TILE // CHUNK)
        ],
        axis=0,
    )
    summed = lax.dot_general(
        left,
        jnp.concatenate([hot, hot], axis=1),
        (((1,), (1,)), ((), ())),
        preferred_element_type=jnp.float32,
    )
    for c in range(TILE // CHUNK):
        at = pl.ds(pl.multiple_of(tile * TILE + c * CHUNK, CHUNK), CHUNK)
        out[:, at] += summed[c * rank : (c + 1) * rank]


def step(
    place,
    mask,
    left,
    right,
    stencil_left,
    weights_left,
    stencil_right,
    weights_right,
    rows,
    cols,
    values,
    left_out,
    right_out,
    left_table,
    right_table,
    *,
    eta,
):
    rank = left.shape[0]
    tile_rows, tile_cols, samples = rows.shape
    for a in range(tile_rows):
        interpolate(
            left, stencil_left, weights_left, left_table, left_out, place[0], place[1], place[2], a
        )
    for b in range(tile_cols):
        interpolate(
            right, stencil_right, weights_right, right_table, right_out, place[3], place[4], place[5], b
        )

    def visit(a, b):
        @pl.when(mask[a, b] != 0)
        def _():
            scale = mask[a, b].astype(jnp.float32) * (-eta)

            def batch(i, _):
                for_left, for_right, at_rows, at_cols = [], [], [], []
                for j in range(ADD // READ):
                    at = pl.ds(pl.multiple_of(i * ADD + j * READ, READ), READ)
                    row = rows[a, b : b + 1, at]
                    col = cols[a, b : b + 1, at]
                    left_cols = read(left_table[a], row, rank)
                    right_cols = read(right_table[b], col, rank)
                    product = jnp.sum(left_cols * right_cols, axis=0, keepdims=True)
                    error = scale * (product - values[a, b : b + 1, at])
                    for_left.append(error * right_cols)
                    for_right.append(error * left_cols)
                    at_rows.append(row)
                    at_cols.append(col)
                join = functools.partial(jnp.concatenate, axis=1)
                add(left_out, join(for_left), join(at_rows), a)
                add(right_out, join(for_right), join(at_cols), b)
                return 0

            lax.fori_loop(0, samples // ADD, batch, 0)

    for b in range(tile_cols):

        def over_rows(a, _, b=b):
            visit(a, b)
            return 0

        lax.fori_loop(0, tile_rows, over_rows, 0)


def on_device(
    coarse_left,
    coarse_right,
    stencil_left,
    weights_left,
    stencil_right,
    weights_right,
    tile_mask,
    sample_rows,
    sample_cols,
    sample_values,
):
    row, col = lax.axis_index("row"), lax.axis_index("col")
    left = lax.all_gather(with_edges(coarse_left, "row"), "col", axis=0, tiled=True)
    right = lax.all_gather(with_edges(coarse_right, "col"), "row", axis=0, tiled=True)
    left_rank, right_rank = coarse_left.shape[0], coarse_right.shape[0]
    place = jnp.stack(
        [
            col * left_rank,
            (col + 1) * left_rank,
            row * coarse_left.shape[1],
            row * right_rank,
            (row + 1) * right_rank,
            col * coarse_right.shape[1],
        ]
    ).astype(jnp.int32)
    rank = left.shape[0]
    tile_rows, tile_cols, _ = sample_rows.shape
    smem = pl.BlockSpec(memory_space=pltpu.SMEM)
    vmem = pl.BlockSpec(memory_space=pltpu.VMEM)
    table = (TILE // CHUNK * rank, 2 * CHUNK)
    left_out, right_out = pl.pallas_call(
        functools.partial(step, eta=4.0 * TILE / (SPT * TILES)),
        out_shape=(
            jax.ShapeDtypeStruct((rank, tile_rows * TILE), jnp.float32),
            jax.ShapeDtypeStruct((rank, tile_cols * TILE), jnp.float32),
        ),
        in_specs=[smem, smem] + [vmem] * 9,
        out_specs=(vmem, vmem),
        scratch_shapes=[
            pltpu.VMEM((tile_rows,) + table, jnp.bfloat16),
            pltpu.VMEM((tile_cols,) + table, jnp.bfloat16),
        ],
        compiler_params=pltpu.CompilerParams(vmem_limit_bytes=60 * 1024 * 1024),
    )(
        place,
        tile_mask,
        left,
        right,
        stencil_left.reshape(-1, 8, 128),
        weights_left,
        stencil_right.reshape(-1, 8, 128),
        weights_right,
        sample_rows,
        sample_cols,
        sample_values,
    )
    cols, rows = lax.axis_size("col"), lax.axis_size("row")
    left_parts = lax.all_to_all(
        left_out.reshape(cols, left_rank, -1), "col", 0, 0, tiled=False
    )
    right_parts = lax.all_to_all(
        right_out.reshape(rows, right_rank, -1), "row", 0, 0, tiled=False
    )
    return (jnp.sum(left_parts, axis=0), jnp.sum(right_parts, axis=0))


def solution(mesh):
    in_specs = (
        P("col", "row"),
        P("row", "col"),
        P("row"),
        P(None, "row"),
        P("col"),
        P(None, "col"),
        P("row", "col"),
        P("row", "col", None),
        P("row", "col", None),
        P("row", "col", None),
    )
    out_specs = (P("col", "row"), P("row", "col"))
    return jax.shard_map(
        on_device, mesh=mesh, in_specs=in_specs, out_specs=out_specs, check_vma=False
    )
```

time: 964 us -> 157 us (0.16)
  local copies, waits for them, and re-layouts: 489 us -> 9.42 us
  other arithmetic: 310 us -> 1.9 us
  waiting for transfers between devices: 139 us -> 60.1 us
  Pallas kernels: 0 us -> 36.8 us
  blocking collectives: 0 us -> 26.6 us
  between operations: 15.4 us -> 0.7 us
  starting transfers between devices: 9.23 us -> 23 us
    gather x10 -> x0, local copies, waits for them, and re-layouts: 448 us -> none  [the longest x2 326 us: spread(): values = jnp.take(padded, columns_at, axis=1)]
    scatter-add x8 -> x0, other arithmetic: 246 us -> none  [the longest x4 127 us: visit(): grad_left = grad_left.at[:, rows_here].add(error[None, :] * right_cols)]
    unnamed x6 -> x0, waiting for transfers between devices: 109 us -> none
    all_to_all x0 -> x2, waiting for transfers between devices: none -> 60.1 us  [the longest x1 48.3 us: on_device(): lax.all_to_all(left_out.reshape(cols, left_rank, -1), 'col', 0, 0, tiled=...]
    reduce_sum x6 -> x2, other arithmetic: 57.4 us -> 1.9 us  [on_device(): return (jnp.sum(left_parts, axis=0), jnp.sum(right_parts, axis=0))]
    pallas_call x0 -> x1, Pallas kernels: none -> 36.8 us  [on_device(): pl.pallas_call(functools.partial(step, eta=4.0 * TILE / (SPT * TILES)), o...]
    all_gather x2 -> x0, waiting for transfers between devices: 30 us -> none  [the longest x1 30 us: on_device(): fine_left = lax.all_gather(left_own, 'col', axis=0, tiled=True)]
    all_gather x0 -> x2, blocking collectives: none -> 26.6 us  [the longest x1 16 us: on_device(): lax.all_gather(with_edges(coarse_left, 'row'), 'col', axis=0, tiled=True)]
  transfers between devices with their start and end apart: 8 -> 6, of which waited for: 3 -> 2; matrix products, arithmetic and copies ran while one was open for 28% -> 5% of each run, Pallas kernels for 0% -> 0%
where the time goes in v1:
time: 157 us; the launch traced here: 158 us
  waiting for transfers between devices  60.1 us (38%)
  Pallas kernels  36.8 us (23%)
  blocking collectives  26.6 us (17%)
  starting transfers between devices  23 us (15%)
  local copies, waits for them, and re-layouts  9.42 us (6%)
  other arithmetic  1.9 us (1%)
    all_to_all x1, waiting for transfers between devices, on_device(): lax.all_to_all(left_out.reshape(cols, left_rank, -1), 'col', 0, 0, tiled=...  48.3 us
    pallas_call x1, Pallas kernels, on_device(): pl.pallas_call(functools.partial(step, eta=4.0 * TILE / (SPT * TILES)), o...  36.8 us
    all_gather x1, blocking collectives, on_device(): lax.all_gather(with_edges(coarse_left, 'row'), 'col', axis=0, tiled=True)  16 us
    all_to_all x1, waiting for transfers between devices, on_device(): lax.all_to_all(right_out.reshape(rows, right_rank, -1), 'row', 0, 0, tile...  11.8 us
    all_gather x1, blocking collectives, on_device(): lax.all_gather(with_edges(coarse_right, 'col'), 'row', axis=0, tiled=True)  10.6 us
    ppermute x2, starting transfers between devices, with_edges(): low = lax.ppermute(block[:, width - LOW:], axis, forward)  8.51 us
    all_to_all x1, starting transfers between devices, on_device(): lax.all_to_all(right_out.reshape(rows, right_rank, -1), 'row', 0, 0, tile...  6.69 us
    all_to_all x1, starting transfers between devices, on_device(): lax.all_to_all(left_out.reshape(cols, left_rank, -1), 'col', 0, 0, tiled=...  5.21 us
  transfers between devices with their start and end apart: 6, of which 2 were waited for; matrix products, arithmetic and copies ran while one was open for 5% of the time, Pallas kernels for 0%

profile of v1, /device:TPU:0, one launch (start us, length us, event | category | flops | bytes accessed | tf_op | source)
XLA Modules:
  0.0 158.5 jit_solution(13282059426767529443)
XLA Ops:
  0.6 0.7 slice.13
  1.3 1.3 collective-permute-start.1
  2.6 0.8 slice.12
  3.4 5.5 %collective-permute-start = (f32[4,2]{1,0:T(4,128)S(1)}, f32[4,2]{1,0:T(4,128)S(1)}, u32[]{:S(2)}, u32[]{:S(2)}) collective-permute-start(f32[4,2]{1,0:T(4,128)S(1)} %slice.12), channel_id=1, source_target_pairs={{0,8},{8,16},{16,24},{1,9},{9,17},{17,25},{2,10},{10,18},{18,26},{... | collective-permute-start | bytes 104 | tf_op jit(solution)/shard_map/ppermute | solution.py:26
  8.9 0.7 slice.15
  9.5 1.3 collective-permute-start.3
  10.8 0.8 slice.14
  11.6 3.0 %collective-permute-start.2 = (f32[8,2]{1,0:T(8,128)S(1)}, f32[8,2]{1,0:T(8,128)S(1)}, u32[]{:S(2)}, u32[]{:S(2)}) collective-permute-start(f32[8,2]{1,0:T(8,128)S(1)} %slice.14), channel_id=1, source_target_pairs={{0,1},{1,2},{2,3},{3,4},{4,5},{5,6},{6,7},{8,9},{9,10},{10,11},{11... | collective-permute-start | bytes 200 | tf_op jit(solution)/shard_map/ppermute | solution.py:26
  14.6 1.3 copy.13.mask
  16.0 0.7 stack.27.place
  16.6 0.0 collective-permute-done
  16.6 0.0 collective-permute-done.1
  16.6 1.0 concatenate.6
  17.6 16.0 %all-gather = f32[8,4,4224]{2,1,0:T(4,128)S(1)} all-gather(f32[1,4,4224]{2,1,0:T(4,128)S(1)} %bitcast.11), channel_id=1, replica_groups=mesh['row'=4,'col'=8] {'col'}, dimensions={0}, use_global_device_ids=true | all-gather | bytes 608256 | tf_op jit(solution)/shard_map/all_gather | solution.py:188
  33.6 1.0 reshape.21.left
  34.6 0.0 collective-permute-done.2
  34.6 0.0 collective-permute-done.3
  34.6 0.9 concatenate.7
  35.5 10.6 %all_gather.7.right = f32[32,2176]{1,0:T(8,128)} all-gather(f32[8,2176]{1,0:T(8,128)S(1)} %concatenate.7), channel_id=1, replica_groups=mesh['row'=4,'col'=8] {'row'}, dimensions={0}, use_global_device_ids=true | all-gather | bytes 348160 | tf_op jit(solution)/shard_map/all_gather | solution.py:189
  46.2 36.8 %shard_map.113 = (f32[32,16384]{1,0:T(8,128)}, f32[32,8192]{1,0:T(8,128)}) custom-call(s32[6]{0:T(128)} %stack.27.place, s32[4,2]{1,0:T(4,128)} %copy.13.mask, f32[32,4224]{1,0:T(8,128)} %reshape.21.left, f32[32,2176]{1,0:T(8,128)} %all_gather.7.right, s32[16,8,128]{2,1,0:T(8,128)} %bitcast.12, f32[4,16384]{1,0:T(4,128)} %weights_left.1, ...), custom_call_target="tpu_custom_call" | custom-call | tf_op jit(solution)/shard_map/pallas_call | solution.py:206
  82.9 0.0 copy-start
  82.9 6.7 %all-to-all-start.1 = ((f32[4,8,8192]{2,1,0:T(8,128)}), f32[4,8,8192]{2,1,0:T(8,128)S(1)}, u32[]{:S(2)}, u32[]{:S(2)}) async-start(f32[4,8,8192]{2,1,0:T(8,128)} %bitcast.10), calls=%async_computation.1 | async-start | bytes 2097152 | tf_op jit(solution)/shard_map/all_to_all | solution.py:236
  89.6 0.0 copy-done
  89.6 1.6 %reshape.18 = f32[8,4,16384]{2,1,0:T(4,128)} reshape(f32[32,16384]{1,0:T(8,128)S(1)} %copy-done) | data formatting | bytes 4194304 | tf_op jit(solution)/shard_map/reshape | solution.py:234
  91.3 11.8 %all-to-all-done.1 = f32[4,8,8192]{2,1,0:T(8,128)S(1)} async-done(((f32[4,8,8192]{2,1,0:T(8,128)}), f32[4,8,8192]{2,1,0:T(8,128)S(1)}, u32[]{:S(2)}, u32[]{:S(2)}) %all-to-all-start.1) | async-done | bytes 1048608 | tf_op jit(solution)/shard_map/all_to_all | solution.py:236
  103.1 5.2 %all-to-all-start = ((f32[8,4,16384]{2,1,0:T(4,128)}), f32[8,4,16384]{2,1,0:T(4,128)S(1)}, u32[]{:S(2)}, u32[]{:S(2)}) async-start(f32[8,4,16384]{2,1,0:T(4,128)} %reshape.18), calls=%async_computation | async-start | bytes 4194304 | tf_op jit(solution)/shard_map/all_to_all | solution.py:233
  108.3 0.8 reduce_sum.19
  109.1 48.3 %all-to-all-done = f32[8,4,16384]{2,1,0:T(4,128)S(1)} async-done(((f32[8,4,16384]{2,1,0:T(4,128)}), f32[8,4,16384]{2,1,0:T(4,128)S(1)}, u32[]{:S(2)}, u32[]{:S(2)}) %all-to-all-start) | async-done | bytes 2097184 | tf_op jit(solution)/shard_map/all_to_all | solution.py:233
  157.3 1.1 reduce_sum.18
  (2 shorter events, 0.0 us)
Async XLA Ops:
  1.3 15.3 %collective-permute-start.1 = (f32[4,3]{1,0:T(4,128)S(1)}, f32[4,3]{1,0:T(4,128)S(1)}, u32[]{:S(2)}, u32[]{:S(2)}) collective-permute-start(f32[4,3]{1,0:T(4,128)S(1)} %slice.13), channel_id=1, source_target_pairs={{8,0},{16,8},{24,16},{9,1},{17,9},{25,17},{10,2},{18,10},{26,18},{... | collective-permute-start | bytes 152 | tf_op jit(solution)/shard_map/ppermute | solution.py:27
  3.4 13.3 %collective-permute-start = (f32[4,2]{1,0:T(4,128)S(1)}, f32[4,2]{1,0:T(4,128)S(1)}, u32[]{:S(2)}, u32[]{:S(2)}) collective-permute-start(f32[4,2]{1,0:T(4,128)S(1)} %slice.12), channel_id=1, source_target_pairs={{0,8},{8,16},{16,24},{1,9},{9,17},{17,25},{2,10},{10,18},{18,26},{... | collective-permute-start | bytes 104 | tf_op jit(solution)/shard_map/ppermute | solution.py:26
  9.5 25.0 %collective-permute-start.3 = (f32[8,3]{1,0:T(8,128)S(1)}, f32[8,3]{1,0:T(8,128)S(1)}, u32[]{:S(2)}, u32[]{:S(2)}) collective-permute-start(f32[8,3]{1,0:T(8,128)S(1)} %slice.15), channel_id=1, source_target_pairs={{1,0},{2,1},{3,2},{4,3},{5,4},{6,5},{7,6},{9,8},{10,9},{11,10},{12... | collective-permute-start | bytes 296 | tf_op jit(solution)/shard_map/ppermute | solution.py:27
  11.6 23.0 %collective-permute-start.2 = (f32[8,2]{1,0:T(8,128)S(1)}, f32[8,2]{1,0:T(8,128)S(1)}, u32[]{:S(2)}, u32[]{:S(2)}) collective-permute-start(f32[8,2]{1,0:T(8,128)S(1)} %slice.14), channel_id=1, source_target_pairs={{0,1},{1,2},{2,3},{3,4},{4,5},{5,6},{6,7},{8,9},{9,10},{10,11},{11... | collective-permute-start | bytes 200 | tf_op jit(solution)/shard_map/ppermute | solution.py:26
  82.9 6.7 %copy-start = (f32[32,16384]{1,0:T(8,128)S(1)}, f32[32,16384]{1,0:T(8,128)}, u32[]{:S(2)}) copy-start(f32[32,16384]{1,0:T(8,128)} %get-tuple-element.4) | copy-start | bytes 6291460
  82.9 20.1 %all-to-all-start.1 = ((f32[4,8,8192]{2,1,0:T(8,128)}), f32[4,8,8192]{2,1,0:T(8,128)S(1)}, u32[]{:S(2)}, u32[]{:S(2)}) async-start(f32[4,8,8192]{2,1,0:T(8,128)} %bitcast.10), calls=%async_computation.1 | async-start | bytes 2097152 | tf_op jit(solution)/shard_map/all_to_all | solution.py:236
  103.1 54.2 %all-to-all-start = ((f32[8,4,16384]{2,1,0:T(4,128)}), f32[8,4,16384]{2,1,0:T(4,128)S(1)}, u32[]{:S(2)}, u32[]{:S(2)}) async-start(f32[8,4,16384]{2,1,0:T(4,128)} %reshape.18), calls=%async_computation | async-start | bytes 4194304 | tf_op jit(solution)/shard_map/all_to_all | solution.py:233
